TPU v7x, 256 devices: a 4x2x16 block of a 4x16x16 slice. The times are simulated.
256 devices in a mesh: groups: 2 (over y), freq: 128 (over z, x, core).
Axes of the slice: x: 4, y: 2, z: 16, core: 2. Of those that a mesh axis runs over, the one named last changes fastest.
The devices are a block of a 4x16x16 slice.
Arguments:
- primary_one: bfloat16 [1024, 512, 512], P(('groups', 'freq')), parts along dimension 0, may hold values from -6 to 6
- primary_two: bfloat16 [1024, 512, 512], P(('groups', 'freq')), parts along dimension 0, may hold values from -6 to 6
- primary_three: bfloat16 [1024, 512, 512], P(('groups', 'freq')), parts along dimension 0, may hold values from -6 to 6
- window_start: int32 [3, 1024, 512], P(None, ('groups', 'freq')), parts along dimension 1, may hold values from 0 to 255
- window_end: int32 [3, 1024, 512], P(None, ('groups', 'freq')), parts along dimension 1, may hold values from 257 to 512
Outputs:
- predicted: bfloat16 [1024, 512, 512], P(('groups', 'freq')), parts along dimension 0
There are 2 independent parts, one for each index of `groups`. A program takes and returns all parts, laid end to end along the dimension named above; each array names one. Nothing has to cross between parts.
Inputs may be any that keep to these rules, and one draw needn't show every extreme that they name: window_start of a trace is below its window_end.
All inputs are finite; a program needn't handle non-finite values.
Results may differ from a plain program's by a relative error of at most 0.0089.
Values may be sent and summed in bfloat16 or wider, within the bound.
No kernel may reach another device: no remote copies, remote signals or barrier semaphores. Data moves between devices by JAX's collectives and lax.ppermute only.
A program may use at most 64 MiB of HBM per device.

v0:
```python
import jax
import jax.numpy as jnp
from jax import lax
from jax.sharding import PartitionSpec as P

F_DEV = 1


def sent_together(arrays, axis, split_dim, concat_dim, along):
    widths = [a.shape[along] for a in arrays]
    both = jnp.concatenate(arrays, axis=along)
    whole = lax.all_to_all(both, axis, split_axis=split_dim, concat_axis=concat_dim, tiled=True)
    return tuple(jnp.split(whole, [sum(widths[:k]) for k in range(1, len(widths))], axis=along))


def make_table(count, samples):
    waves = jnp.arange(1, count + 1, dtype=jnp.int32)[:, None]
    times = jnp.arange(samples, dtype=jnp.int32)[None, :]
    phase = waves * times % samples
    angle = 2.0 * jnp.pi / samples * phase.astype(jnp.float32)
    both = jnp.stack([jnp.cos(angle), -jnp.sin(angle)], axis=1)
    return both.reshape(2 * count, samples).astype(jnp.bfloat16)


def spectrum(traces, start, finish, table, count):
    sources, receivers, samples = traces.shape
    times = jnp.arange(samples, dtype=jnp.int32)
    inside = (times >= start[:, :, None]) & (times < finish[:, :, None])
    windowed = jnp.where(inside, traces, jnp.zeros_like(traces))
    flat = windowed.reshape(sources * receivers, samples)
    spec = lax.dot_general(
        table, flat, (((1,), (1,)), ((), ())), preferred_element_type=jnp.float32
    )
    spec = spec * (1.0 / jnp.sqrt(jnp.float32(samples)))
    return spec.astype(jnp.bfloat16).reshape(count, 2, sources, receivers)


def correlate(first, second):
    swapped = jnp.stack([first[:, 1], -first[:, 0]], axis=1)
    left = jnp.stack([first, swapped], axis=1)
    cross = jnp.einsum("fkcsr,fcur->fksu", left, second, preferred_element_type=jnp.float32)
    cross = cross * (1.0 / jnp.sqrt(jnp.float32(first.shape[3])))
    return cross.astype(jnp.bfloat16)


def convolve(cross, third):
    right = jnp.stack(
        [
            jnp.stack([third[:, 0], -third[:, 1]], axis=1),
            jnp.stack([third[:, 1], third[:, 0]], axis=1),
        ],
        axis=1,
    )
    multiple = jnp.einsum("fcsu,fkcur->fksr", cross, right, preferred_element_type=jnp.float32)
    multiple = multiple * (1.0 / jnp.sqrt(jnp.float32(third.shape[2])))
    return multiple.astype(jnp.bfloat16)


def on_device(primary_one, primary_two, primary_three, window_start, window_end):
    samples = primary_one.shape[2]
    count = F_DEV * lax.axis_size("freq")
    table = make_table(count, samples)
    spec_one = spectrum(primary_one, window_start[0], window_end[0], table, count)
    spec_two = spectrum(primary_two, window_start[1], window_end[1], table, count)
    spec_three = spectrum(primary_three, window_start[2], window_end[2], table, count)
    first, second = sent_together((spec_one, spec_two), "freq", 0, 2, 1)
    cross = correlate(first, second)
    third = lax.all_to_all(spec_three, "freq", split_axis=0, concat_axis=2, tiled=True)
    multiple = convolve(cross, third)
    piece = lax.all_to_all(multiple, "freq", split_axis=2, concat_axis=0, tiled=True)
    waves, parts, sources, receivers = piece.shape
    flat = piece.reshape(waves * parts, sources * receivers)
    timed = lax.dot_general(
        flat, table, (((0,), (0,)), ((), ())), preferred_element_type=jnp.float32
    )
    timed = timed * (1.0 / jnp.sqrt(jnp.float32(count)))
    return timed.astype(jnp.bfloat16).reshape(sources, receivers, samples)


def solution(mesh):
    return jax.shard_map(
        on_device,
        mesh=mesh,
        in_specs=(
            P(("groups", "freq"), None, None),
            P(("groups", "freq"), None, None),
            P(("groups", "freq"), None, None),
            P(None, ("groups", "freq"), None),
            P(None, ("groups", "freq"), None),
        ),
        out_specs=P(("groups", "freq"), None, None),
        check_vma=False,
    )
```

profile of v0, /device:TPU:35, one launch (start us, length us, event | category | flops | bytes accessed | tf_op | source)
XLA Modules:
  0.0 282.8 jit_solution(12625566358384556773)
XLA Ops:
  0.0 0.7 slice_bitcast_fusion.3
  0.7 0.7 slice_bitcast_fusion.2
  1.5 1.2 cosine_convert_fusion
  2.7 0.3 copy.36
  3.0 0.1 convert_element_type.64
  3.1 4.2 %fusion.1 = (bf16[4,512,512]{2,1,0:T(8,128)(2,1)S(1)}, bf16[4,512,512]{2,1,0:T(8,128)(2,1)S(1)}) fusion(bf16[4,512,512]{2,1,0:T(8,128)(2,1)} %param.7, s32[4,512]{1,0:T(4,128)S(1)} %get-tuple-element.17, s32[4,512]{1,0:T(4,128)S(1)} %get-tuple-element.14, bf16[4,512,512]{2,1,0:T(8,128)(2,1)} %param.5, s32[4,512]{1,0:T(4,128)S(1)} %get-tuple-element.16, ...), kind=kLoop, calls=%fused_computation.8 | loop fusion | flops 8388608 | bytes 8421376 | tf_op jit(solution)/shard_map/jit(_where)/select_n | solution.py:29
  7.3 1.7 fusion.6
  9.0 1.8 reshape.176
  10.9 1.8 copy.37
  12.7 30.2 %all-to-all-start = ((bf16[128,2,4,512]{3,1,2,0:T(2,128)(2,1)}), bf16[128,2,4,512]{3,1,2,0:T(2,128)(2,1)S(1)}, u32[]{:S(2)}, u32[]{:S(2)}) async-start(bf16[128,2,4,512]{3,1,2,0:T(2,128)(2,1)} %copy.37), calls=%async_computation | async-start | bytes 2097152 | tf_op jit(solution)/shard_map/all_to_all | solution.py:68
  42.9 1.7 fusion.7
  44.6 1.8 reshape.179
  46.5 0.0 copy-start
  46.5 0.8 copy.40
  47.3 0.7 copy-done
  48.1 1.2 fusion.5
  49.3 1.7 fusion.8
  51.0 1.8 reshape.181
  52.9 0.8 copy.41
  53.7 3.2 %pad_maximum_fusion = bf16[128,4,4,512]{3,1,2,0:T(4,128)(2,1)} fusion(bf16[128,2,4,512]{3,1,2,0:T(2,128)(2,1)S(1)} %copy.41, bf16[128,2,4,512]{3,1,2,0:T(2,128)(2,1)S(1)} %copy.40), kind=kLoop, calls=%fused_computation.23 | loop fusion | flops 4194304 | bytes 4194304 | tf_op jit(solution)/shard_map/concatenate | solution.py:11
  56.9 39.6 %all-to-all-done = bf16[128,2,4,512]{3,1,2,0:T(2,128)(2,1)S(1)} async-done(((bf16[128,2,4,512]{3,1,2,0:T(2,128)(2,1)}), bf16[128,2,4,512]{3,1,2,0:T(2,128)(2,1)S(1)}, u32[]{:S(2)}, u32[]{:S(2)}) %all-to-all-start) | async-done | bytes 1048608 | tf_op jit(solution)/shard_map/all_to_all | solution.py:68
  96.5 9.1 %all-to-all-start.1 = ((bf16[128,4,4,512]{3,1,2,0:T(4,128)(2,1)}), bf16[128,4,4,512]{3,1,2,0:T(4,128)(2,1)S(1)}, u32[]{:S(2)}, u32[]{:S(2)}) async-start(bf16[128,4,4,512]{3,1,2,0:T(4,128)(2,1)} %pad_maximum_fusion), calls=%async_computation.1 | async-start | bytes 4194304 | tf_op jit(solution)/shard_map/all_to_all | solution.py:12
  105.7 2.5 fusion.30
  108.2 2.3 copy.51
  110.5 0.9 neg.23
  111.4 2.3 copy.50
  113.7 2.6 maximum_bitcast_fusion.12
  116.3 86.3 %all-to-all-done.1 = bf16[128,4,4,512]{3,1,2,0:T(4,128)(2,1)S(1)} async-done(((bf16[128,4,4,512]{3,1,2,0:T(4,128)(2,1)}), bf16[128,4,4,512]{3,1,2,0:T(4,128)(2,1)S(1)}, u32[]{:S(2)}, u32[]{:S(2)}) %all-to-all-start.1) | async-done | bytes 2097184 | tf_op jit(solution)/shard_map/all_to_all | solution.py:12
  202.6 1.5 fusion.29
  204.1 2.3 fusion.28
  206.4 0.1 copy.53
  206.5 0.1 copy_negate_fusion
  206.6 0.0 copy-start.1
  206.6 0.0 copy-start.2
  206.6 0.2 copy.63
  206.8 1.1 maximum_bitcast_fusion.14
  207.9 0.0 copy-done.1
  207.9 0.7 copy-done.2
  208.5 4.9 %fusion.18 = bf16[1,2,512,512]{2,3,1,0:T(8,128)(2,1)} fusion(bf16[1,1,2,512,512]{3,4,2,1,0:T(8,128)(2,1)S(1)} %copy-done.2, bf16[1,1,2,512,512]{3,4,2,1,0:T(8,128)(2,1)S(1)} %copy-done.1, bf16[1,1,2,512,512]{4,3,2,1,0:T(8,128)(2,1)} %maximum_bitcast_fusion.14, bf16[1,1,2,512,512]{4,3,2,1,0:T(8,128)(2,1)S(1)} %bitcast.104, ...), kind=kOutput, calls=%fused_computation.33 | convolution fusion | flops 2151677952 | bytes 6291456 | tf_op jit(solution)/shard_map/fcsu,fkcur->fksr/dot_general | solution.py:54
  213.4 2.5 copy.46
  215.9 64.1 %all_to_all.51 = bf16[1,2,512,512]{3,1,0,2:T(2,128)(2,1)S(1)} all-to-all(bf16[1,2,512,512]{3,1,0,2:T(2,128)(2,1)S(1)} %copy.46), channel_id=1, replica_groups=mesh['groups'=2,'freq'=128] {'freq'}, dimensions={2} | all-to-all | bytes 2097152 | tf_op jit(solution)/shard_map/all_to_all | solution.py:70
  280.1 0.4 copy.47
  280.5 0.3 copy.56
  280.8 2.1 multiply_convert_fusion
  (2 shorter events, 0.0 us)
Async XLA Ops:
  12.7 83.8 %all-to-all-start = ((bf16[128,2,4,512]{3,1,2,0:T(2,128)(2,1)}), bf16[128,2,4,512]{3,1,2,0:T(2,128)(2,1)S(1)}, u32[]{:S(2)}, u32[]{:S(2)}) async-start(bf16[128,2,4,512]{3,1,2,0:T(2,128)(2,1)} %copy.37), calls=%async_computation | async-start | bytes 2097152 | tf_op jit(solution)/shard_map/all_to_all | solution.py:68
  46.5 1.6 copy-start
  96.5 106.1 %all-to-all-start.1 = ((bf16[128,4,4,512]{3,1,2,0:T(4,128)(2,1)}), bf16[128,4,4,512]{3,1,2,0:T(4,128)(2,1)S(1)}, u32[]{:S(2)}, u32[]{:S(2)}) async-start(bf16[128,4,4,512]{3,1,2,0:T(4,128)(2,1)} %pad_maximum_fusion), calls=%async_computation.1 | async-start | bytes 4194304 | tf_op jit(solution)/shard_map/all_to_all | solution.py:12
  206.6 1.3 copy-start.1
  206.6 1.9 copy-start.2
where the time goes:
time: 284 us; the launch traced here: 283 us
  waiting for transfers between devices  126 us (44%)
  blocking collectives  64.1 us (23%)
  starting transfers between devices  39.4 us (14%)
  local copies, waits for them, and re-layouts  26.7 us (9%)
  other arithmetic  14.5 us (5%)
  matrix products  12.1 us (4%)
    all_to_all x1, waiting for transfers between devices, sent_together(): lax.all_to_all(both, axis, split_axis=split_dim, concat_axis=concat_dim,...  86.3 us
    all_to_all x1, blocking collectives, on_device(): lax.all_to_all(multiple, 'freq', split_axis=2, concat_axis=0, tiled=True)  64.1 us
    all_to_all x1, waiting for transfers between devices, on_device(): lax.all_to_all(spec_three, 'freq', split_axis=0, concat_axis=2, tiled=True)  39.6 us
    all_to_all x1, starting transfers between devices, on_device(): lax.all_to_all(spec_three, 'freq', split_axis=0, concat_axis=2, tiled=True)  30.2 us
    all_to_all x1, starting transfers between devices, sent_together(): lax.all_to_all(both, axis, split_axis=split_dim, concat_axis=concat_dim,...  9.15 us
    reshape x6, local copies, waits for them, and re-layouts, spectrum(): return spec.astype(jnp.bfloat16).reshape(count, 2, sources, receivers)  9.02 us
    unnamed x11, local copies, waits for them, and re-layouts  6.66 us
  transfers between devices with their start and end apart: 2, of which 2 were waited for; matrix products, arithmetic and copies ran while one was open for 8% of the time, Pallas kernels for 0%

commit v1 on v0

--- a/solution.py
+++ b/solution.py
@@ -65,7 +65,12 @@
     spec_three = spectrum(primary_three, window_start[2], window_end[2], table, count)
     first, second = sent_together((spec_one, spec_two), "freq", 0, 2, 1)
     cross = correlate(first, second)
-    third = lax.all_to_all(spec_three, "freq", split_axis=0, concat_axis=2, tiled=True)
+    third = jnp.concatenate(
+        lax.all_to_all(
+            jnp.stack(jnp.split(spec_three, lax.axis_size("freq"), axis=0)), "freq", 0, 0
+        ),
+        axis=2,
+    )
     multiple = convolve(cross, third)
     piece = lax.all_to_all(multiple, "freq", split_axis=2, concat_axis=0, tiled=True)
     waves, parts, sources, receivers = piece.shape

time: 284 us -> 357 us (1.26)
  local copies, waits for them, and re-layouts: 26.7 us -> 101 us
    unnamed x11 -> x138, local copies, waits for them, and re-layouts: 6.66 us -> 82.9 us
    reshape x6 -> x4, local copies, waits for them, and re-layouts: 9.02 us -> 5.35 us  [spectrum(): return spec.astype(jnp.bfloat16).reshape(count, 2, sources, receivers)]
  transfers between devices with their start and end apart: 2 -> 2, of which waited for: 2 -> 2; matrix products, arithmetic and copies ran while one was open for 8% -> 7% of each run, Pallas kernels for 0% -> 0%
where the time goes in v1:
time: 357 us; the launch traced here: 356 us
  waiting for transfers between devices  126 us (35%)
  local copies, waits for them, and re-layouts  101 us (28%)
  blocking collectives  64.1 us (18%)
  starting transfers between devices  39.4 us (11%)
  other arithmetic  14.4 us (4%)
  matrix products  11.1 us (3%)
    all_to_all x1, waiting for transfers between devices, sent_together(): lax.all_to_all(both, axis, split_axis=split_dim, concat_axis=concat_dim,...  86.3 us
    unnamed x138, local copies, waits for them, and re-layouts  82.9 us
    all_to_all x1, blocking collectives, on_device(): lax.all_to_all(multiple, 'freq', split_axis=2, concat_axis=0, tiled=True)  64.1 us
    all_to_all x1, waiting for transfers between devices, on_device(): lax.all_to_all(jnp.stack(jnp.split(spec_three, lax.axis_size('freq'), axi...  39.6 us
    all_to_all x1, starting transfers between devices, on_device(): lax.all_to_all(jnp.stack(jnp.split(spec_three, lax.axis_size('freq'), axi...  30.2 us
    all_to_all x1, starting transfers between devices, sent_together(): lax.all_to_all(both, axis, split_axis=split_dim, concat_axis=concat_dim,...  9.15 us
  transfers between devices with their start and end apart: 2, of which 2 were waited for; matrix products, arithmetic and copies ran while one was open for 7% of the time, Pallas kernels for 0%

profile of v1, /device:TPU:35, one launch (start us, length us, event | category | flops | bytes accessed | tf_op | source)
XLA Modules:
  0.0 356.0 jit_solution(14491896108286407356)
XLA Ops:
  0.0 0.7 slice_bitcast_fusion.3
  0.7 0.7 slice_bitcast_fusion.2
  1.5 1.2 cosine_convert_fusion
  3.1 4.2 %fusion.1 = (bf16[4,512,512]{2,1,0:T(8,128)(2,1)S(1)}, bf16[4,512,512]{2,1,0:T(8,128)(2,1)S(1)}) fusion(bf16[4,512,512]{2,1,0:T(8,128)(2,1)} %param.7, s32[4,512]{1,0:T(4,128)S(1)} %get-tuple-element.145, s32[4,512]{1,0:T(4,128)S(1)} %get-tuple-element.142, bf16[4,512,512]{2,1,0:T(8,128)(2,1)} %param.5, s32[4,512]{1,0:T(4,128)S(1)} %get-tuple-element.144, ...), kind=kLoop, calls=%fused_computation.8 | loop fusion | flops 8388608 | bytes 8421376 | tf_op jit(solution)/shard_map/jit(_where)/select_n | solution.py:29
  7.3 0.7 fusion.6
  9.5 0.6 constant_dynamic-update-slice_fusion.126
  13.7 0.6 constant_dynamic-update-slice_fusion.119
  16.8 0.6 constant_dynamic-update-slice_fusion.114
  22.8 0.6 constant_dynamic-update-slice_fusion.104
  24.0 0.6 constant_dynamic-update-slice_fusion.102
  34.2 0.6 constant_dynamic-update-slice_fusion.85
  49.2 0.6 constant_dynamic-update-slice_fusion.60
  51.6 0.6 constant_dynamic-update-slice_fusion.56
  56.4 0.6 constant_dynamic-update-slice_fusion.48
  57.0 0.6 constant_dynamic-update-slice_fusion.47
  63.0 0.6 constant_dynamic-update-slice_fusion.37
  63.6 0.6 constant_dynamic-update-slice_fusion.36
  64.2 0.6 constant_dynamic-update-slice_fusion.35
  67.2 0.6 constant_dynamic-update-slice_fusion.30
  73.2 0.6 constant_dynamic-update-slice_fusion.20
  76.8 0.6 constant_dynamic-update-slice_fusion.14
  78.6 0.6 constant_dynamic-update-slice_fusion.11
  85.9 30.2 %all-to-all-start = ((bf16[128,1,2,4,512]{4,2,3,1,0:T(2,128)(2,1)}), bf16[128,1,2,4,512]{4,2,3,1,0:T(2,128)(2,1)S(1)}, u32[]{:S(2)}, u32[]{:S(2)}) async-start(bf16[128,1,2,4,512]{4,2,3,1,0:T(2,128)(2,1)} %constant_dynamic-update-slice_fusion), calls=%async_computation | async-start | bytes 2097152 | tf_op jit(solution)/shard_map/all_to_all | solution.py:69
  116.1 1.7 fusion.7
  117.8 1.8 reshape.440
  119.7 0.8 copy.548
  120.5 0.7 copy-done
  121.2 1.2 fusion.5
  122.5 1.7 fusion.8
  124.2 1.8 reshape.442
  126.0 0.8 copy.549
  126.9 3.2 pad_maximum_fusion
  130.1 39.6 %all-to-all-done = bf16[128,1,2,4,512]{4,2,3,1,0:T(2,128)(2,1)S(1)} async-done(((bf16[128,1,2,4,512]{4,2,3,1,0:T(2,128)(2,1)}), bf16[128,1,2,4,512]{4,2,3,1,0:T(2,128)(2,1)S(1)}, u32[]{:S(2)}, u32[]{:S(2)}) %all-to-all-start) | async-done | bytes 1048608 | tf_op jit(solution)/shard_map/all_to_all | solution.py:69
  169.7 9.1 %all-to-all-start.1 = ((bf16[128,4,4,512]{3,1,2,0:T(4,128)(2,1)}), bf16[128,4,4,512]{3,1,2,0:T(4,128)(2,1)S(1)}, u32[]{:S(2)}, u32[]{:S(2)}) async-start(bf16[128,4,4,512]{3,1,2,0:T(4,128)(2,1)} %pad_maximum_fusion), calls=%async_computation.1 | async-start | bytes 4194304 | tf_op jit(solution)/shard_map/all_to_all | solution.py:12
  178.8 2.5 fusion.30
  181.3 2.3 copy.559
  183.6 0.9 neg.23
  184.5 2.3 copy.558
  186.9 2.6 maximum_bitcast_fusion.12
  189.4 86.3 %all-to-all-done.1 = bf16[128,4,4,512]{3,1,2,0:T(4,128)(2,1)S(1)} async-done(((bf16[128,4,4,512]{3,1,2,0:T(4,128)(2,1)}), bf16[128,4,4,512]{3,1,2,0:T(4,128)(2,1)S(1)}, u32[]{:S(2)}, u32[]{:S(2)}) %all-to-all-start.1) | async-done | bytes 2097184 | tf_op jit(solution)/shard_map/all_to_all | solution.py:12
  275.8 1.5 fusion.29
  277.3 2.3 fusion.28
  279.9 1.1 maximum_bitcast_fusion.14
  281.0 0.7 copy-done.2
  281.7 4.9 %fusion.18 = bf16[1,2,512,512]{2,3,1,0:T(8,128)(2,1)} fusion(bf16[1,1,2,512,512]{3,4,2,1,0:T(8,128)(2,1)S(1)} %copy-done.2, bf16[1,1,2,512,512]{3,4,2,1,0:T(8,128)(2,1)S(1)} %copy-done.1, bf16[1,1,2,512,512]{4,3,2,1,0:T(8,128)(2,1)} %maximum_bitcast_fusion.14, bf16[1,1,2,512,512]{4,3,2,1,0:T(8,128)(2,1)S(1)} %bitcast.230, ...), kind=kOutput, calls=%fused_computation.33 | convolution fusion | flops 2151677952 | bytes 6291456 | tf_op jit(solution)/shard_map/fcsu,fkcur->fksr/dot_general | solution.py:54
  286.6 2.5 copy.554
  289.1 64.1 %all_to_all.38 = bf16[1,2,512,512]{3,1,0,2:T(2,128)(2,1)S(1)} all-to-all(bf16[1,2,512,512]{3,1,0,2:T(2,128)(2,1)S(1)} %copy.554), channel_id=1, replica_groups=mesh['groups'=2,'freq'=128] {'freq'}, dimensions={2} | all-to-all | bytes 2097152 | tf_op jit(solution)/shard_map/all_to_all | solution.py:75
  353.9 2.1 multiply_convert_fusion
  (131 shorter events, 68.8 us)
Async XLA Ops:
  85.9 83.8 %all-to-all-start = ((bf16[128,1,2,4,512]{4,2,3,1,0:T(2,128)(2,1)}), bf16[128,1,2,4,512]{4,2,3,1,0:T(2,128)(2,1)S(1)}, u32[]{:S(2)}, u32[]{:S(2)}) async-start(bf16[128,1,2,4,512]{4,2,3,1,0:T(2,128)(2,1)} %constant_dynamic-update-slice_fusion), calls=%async_computation | async-start | bytes 2097152 | tf_op jit(solution)/shard_map/all_to_all | solution.py:69
  119.6 1.6 copy-start
  169.7 106.1 %all-to-all-start.1 = ((bf16[128,4,4,512]{3,1,2,0:T(4,128)(2,1)}), bf16[128,4,4,512]{3,1,2,0:T(4,128)(2,1)S(1)}, u32[]{:S(2)}, u32[]{:S(2)}) async-start(bf16[128,4,4,512]{3,1,2,0:T(4,128)(2,1)} %pad_maximum_fusion), calls=%async_computation.1 | async-start | bytes 4194304 | tf_op jit(solution)/shard_map/all_to_all | solution.py:12
  279.8 1.3 copy-start.1
  279.8 1.9 copy-start.2
